TPU v7x, 128 devices: a whole 4x4x4 slice. The times are simulated.
128 devices in a mesh: row: 16 (over x, y), col: 8 (over z, core).
Axes of the slice: x: 4, y: 4, z: 4, core: 2. Of those that a mesh axis runs over, the one named last changes fastest.
Arguments:
- weights: int32 [8192, 8192], P('row', 'col'), may hold values from 1 to 64
Outputs:
- distances: int32 [8192, 8192], P('row', 'col')
All inputs are finite; a program needn't handle non-finite values.
Results may differ from a plain program's by a relative error of at most 0.000001.
Values may be sent and summed in bfloat16 or wider, within the bound.
A program may use at most 64 MiB of HBM per device.

v0:
```python
import math

import jax
import jax.numpy as jnp
from jax import lax
from jax.experimental import pallas as pl
from jax.experimental.pallas import tpu as pltpu
from jax.sharding import PartitionSpec as P

F32 = jnp.float32
BF16 = jnp.bfloat16
MESH = pl.DeviceIdType.MESH
ALPHA = 60.25
BETA = 6.2
SHIFT = 0.984
STEP = 2.0**-BETA
B = 128
S = 4


LOG = 1.0 / (BETA * math.log(2.0))
FLOOR = 2 * ALPHA / BETA + SHIFT


def encode(t):
    u = t * 0.5
    half = jnp.floor(u)
    return jnp.exp2(half * -BETA + ALPHA), u > half


def enc_right(t):
    e, odd = encode(t)
    return jnp.where(odd, e * STEP, e).astype(BF16), e.astype(BF16)


def split_left(t):
    e, odd = encode(t)
    odd_floor = jnp.where(odd, e, 0.0)
    return tuple(u.astype(BF16) for u in (odd_floor, jnp.where(odd, 0.0, e), odd_floor * STEP))


def enc_left(t):
    first = jnp.where(lax.broadcasted_iota(jnp.int32, t.shape, 1) < B // 2, 1.0, 0.0)
    pairs = []
    parts = split_left(t)
    for keep in (first.astype(BF16), (1.0 - first).astype(BF16)):
        of, ev, oc = (u * keep for u in parts)
        pairs.append((jnp.concatenate([of, ev], 1), jnp.concatenate([ev, oc], 1)))
    return pairs


def dot(left, right):
    return jnp.dot(left, right, preferred_element_type=F32)


def decode(floors, ceils, bias):
    low = jnp.floor(FLOOR - jnp.log(floors) * LOG)
    high = jnp.floor(FLOOR + bias - jnp.log(ceils) * LOG)
    return low + jnp.minimum(high, low + (1.0 + bias))


def min_plus(left, right, old):
    (f0, c0), (f1, c1) = left
    floors = jnp.maximum(dot(f0, right), dot(f1, right))
    ceils = jnp.maximum(dot(c0, right), dot(c1, right))
    return jnp.minimum(old, decode(floors, ceils, 1.0))


def min_plus_block(block):
    of, ev, oc = split_left(block)
    ceil, floor = enc_right(block)
    none = jnp.zeros((B // 2, B), BF16)
    first = jnp.concatenate([ceil[: B // 2], none, floor[: B // 2], none], 0)
    second = jnp.concatenate([none, ceil[B // 2 :], none, floor[B // 2 :]], 0)
    right = jnp.concatenate([first, second], 1)
    floors = dot(jnp.concatenate([of, ev], 1), right)
    ceils = dot(jnp.concatenate([ev, oc], 1), right)
    floors = jnp.maximum(floors[:, :B], floors[:, B:])
    ceils = jnp.maximum(ceils[:, :B], ceils[:, B:])
    return jnp.minimum(block, decode(floors, ceils, 1.0))


def remote(src, dst, send, recv, where):
    return pltpu.make_async_remote_copy(
        src_ref=src, dst_ref=dst, send_sem=send, recv_sem=recv, device_id=where, device_id_type=MESH
    )


def gather_kernel(
    w_hbm, x_ref, r0, r1, wp, wr, wc, rs, yp, yi, y, enc_row,
    w_sem, p1_send, p1_recv, p2_send, p2_recv, pf_send, yi_send, yi_recv, fi_send,
    s0_send, s0_recv, s1_send, s1_recv, a0_send, a0_recv, a1_send, a1_recv, b0_send, b0_recv, b1_send, b1_recv,
):
    row, col = lax.axis_index("row"), lax.axis_index("col")
    cx, cy = row // S, row % S
    cz, core = col // 2, col % 2
    block_owner = jnp.logical_and(cy == 0, core == 0)

    def at_x(x):
        return {"row": x * S + cy}

    def at_y(v):
        return {"row": cx * S + v}

    def in_slab(d):
        other = (cx * S + cz + d) % 16
        ox, oz = other // S, other % S
        return ox, oz, {"row": ox * S + cy, "col": oz * 2 + core}

    partner = {"col": cz * 2 + (1 - core)}

    barrier = pltpu.get_barrier_semaphore()

    def greet(where):
        pl.semaphore_signal(barrier, inc=1, device_id=where, device_id_type=MESH)

    for d in range(1, S):
        greet(at_y((cy + d) % S))
    for d in range(1, 16):
        greet(in_slab(d)[2])
    greet(partner)

    load_block = pltpu.make_async_copy(w_hbm.at[pl.ds(0, B), pl.ds(0, B)], wp, w_sem.at[0])
    load_rows = pltpu.make_async_copy(w_hbm.at[pl.ds(0, B)], wr, w_sem.at[1])
    load_cols = pltpu.make_async_copy(w_hbm.at[:, pl.ds(0, B)], wc, w_sem.at[2])

    @pl.when(block_owner)
    def _():
        load_block.start()

    @pl.when(cy == 0)
    def _():
        load_rows.start()

    @pl.when(core == 0)
    def _():
        load_cols.start()

    @pl.when(block_owner)
    def _():
        load_block.wait()
        yp[cz, cx] = wp[...].astype(BF16)

    pl.semaphore_wait(barrier, 19)

    def block_y(d):
        return remote(yp.at[cz, cx], yp.at[cz, cx], p1_send.at[d], p1_recv, at_y((cy + d) % S))

    def block_out(d, where):
        return remote(yp.at[cz, cx], yp.at[cz, cx], p2_send.at[d], p2_recv.at[cz * S + cx], where)

    def block_in(ox, oz, send, where):
        return remote(yp.at[oz, ox], yp.at[oz, ox], send, p2_recv.at[oz * S + ox], where)

    def cols_out(d, where):
        return remote(yi.at[cz], yi.at[cz], yi_send.at[d], yi_recv.at[cz], where)

    def cols_in(oz, send):
        return remote(yi.at[oz], yi.at[oz], send, yi_recv.at[oz], partner)

    def scatter(q):
        return (
            remote(rs.at[q, 0], r0.at[q, cx], s0_send.at[q], s0_recv, at_y(q)),
            remote(rs.at[q, 1], r1.at[cx, q], s1_send.at[q], s1_recv, at_y(q)),
        )

    def stage_a(d, x, v):
        return (
            remote(r0.at[cy, x], r0.at[cy, x], a0_send.at[d], a0_recv.at[x], at_x((cx + d) % S)),
            remote(r1.at[cx, v], r1.at[cx, v], a1_send.at[d], a1_recv.at[v], at_y((cy + d) % S)),
        )

    def stage_b(d, x, v):
        return (
            remote(r0.at[v], r0.at[v], b0_send.at[d], b0_recv.at[v], at_y((cy + d) % S)),
            remote(r1.at[x], r1.at[x], b1_send.at[d], b1_recv.at[x], at_x((cx + d) % S)),
        )

    def start_scatter():
        @pl.when(cy == 0)
        def _():
            for q in range(1, S):
                for copy in scatter(q):
                    copy.start()

    def start_a():
        @pl.when(cy != 0)
        def _():
            for copy in scatter(cy):
                copy.wait_recv()

        for d in range(1, S):
            for copy in stage_a(d, cx, cy):
                copy.start()

    def start_b(half):
        for d in range(1, S):
            stage_a(d, (cx + d) % S, (cy + d) % S)[half].wait_recv()
        for d in range(1, S):
            stage_b(d, cx, cy)[half].start()

    @pl.when(block_owner)
    def _():
        for d in range(1, S):
            block_y(d).start()

    @pl.when(core == 0)
    def _():
        load_cols.wait()
        yi[cz] = wc[...].astype(BF16)

    @pl.when(cy == 0)
    def _():
        load_rows.wait()
        for q in range(S):
            for h in range(2):
                rs[q, h] = wr[q * 32 : (q + 1) * 32, h * 512 : (h + 1) * 512].astype(BF16)
        r0[0, cx] = wr[0:32, 0:512].astype(BF16)
        r1[cx, 0] = wr[0:32, 512:1024].astype(BF16)

    @pl.when(core == 0)
    def _():
        for d in range(1, S):
            cols_out(d, {"col": (cz + d) % S * 2}).start()
        cols_out(0, partner).start()
        start_scatter()

        @pl.when(cy != 0)
        def _():
            block_y(0).wait_recv()

        for d in range(1, 16):
            block_out(d, in_slab(d)[2]).start()
        block_out(0, partner).start()
        start_a()
        for d in range(1, S):
            oz = (cz + d) % S
            cols_in(oz, yi_send.at[0]).wait_recv()
            cols_in(oz, fi_send.at[d]).start()

    @pl.when(core == 1)
    def _():
        start_scatter()
        start_a()
        for oz in range(S):
            cols_in(oz, yi_send.at[0]).wait_recv()
        block_in(cx, cz, p2_send.at[0], partner).wait_recv()

    here = cx * S + cz

    def take(d):
        ox, oz, _ = in_slab(d)
        block_in(ox, oz, p2_send.at[0], partner).wait_recv()

        @pl.when(core == 0)
        def _():
            block_in(ox, oz, pf_send.at[d], partner).start()

    def take_other(d):
        @pl.when((here + d) % 16 != 0)
        def _():
            take(d)

    def rows_of(i, count=1):
        return pl.ds(i * B, count * B)

    def column(s, i, count=1):
        return y.at[s // 2, rows_of(i, count), pl.ds(s % 2 * B, B)]

    def update(s, i, which=(0, 1), count=1):
        left = enc_left(column(s, i, count)[...])
        for u in which:
            y[u, rows_of(i, count), :] = min_plus(left, enc_row[s % 2, u], y[u, rows_of(i, count), :])

    def panel(s, block):
        column(s, s)[...] = block
        closed = enc_left(block)
        for u in range(2):
            old = y[u, rows_of(s), :]
            new = min_plus(closed, jnp.concatenate(enc_right(old), 0), old)
            y[u, rows_of(s), :] = new
            ceil, floor = enc_right(new)
            enc_row[s % 2, u, 0:B, :] = ceil
            enc_row[s % 2, u, B : 2 * B, :] = floor

    start_b(0)

    @pl.when(here != 0)
    def _():
        take((16 - here) % 16)

    @pl.when(core == 0)
    def _():
        for d in range(1, 16):
            take_other(d)

    def square_and_take(i, block):
        block = min_plus_block(block)

        @pl.when(core == 1)
        def _():
            for d in range(3):
                take_other(1 + 3 * i + d)

        return block

    block = lax.fori_loop(0, 5, square_and_take, yp[0, 0].astype(F32) - 1.0)
    start_b(1)
    block = min_plus_block(block)

    for t in range(S):
        lanes = slice(t % 2 * B, (t % 2 + 1) * B)
        for s in range(S):
            y[t // 2, s * B : (s + 1) * B, lanes] = yp[t, s].astype(F32) - 1.0
        y[t // 2, S * B :, lanes] = yi[t].astype(F32) - 1.0

    for s in range(S - 1):
        panel(s, block)
        near = (s + 1) // 2
        update(s, s + 1, (near,))
        block = column(s + 1, s + 1)[...]
        rest = [(s + 1, (1 - near,))] + [(i, (0, 1)) for i in range(s + 2, 2 * S)]
        done = 0
        for q in range(6):
            until = -(-len(rest) * (q + 1) // 6)
            for i, which in rest[done:until]:
                update(s, i, which)
            block = min_plus_block(block)
            done = until
    panel(S - 1, block)
    for i in range(S, 2 * S, 4):
        update(S - 1, i, count=4)
    for t in range(S):
        x_ref[t] = y[t // 2, S * B :, t % 2 * B : (t % 2 + 1) * B].astype(BF16)

    for d in range(1, S):
        for copy in stage_b(d, (cx + d) % S, (cy + d) % S):
            copy.wait_recv()

    @pl.when(core == 0)
    def _():
        @pl.when(cy == 0)
        def _():
            for d in range(1, S):
                block_y(d).wait_send()

        for d in range(16):
            block_out(d, partner).wait_send()
        for d in range(S):
            cols_out(d, partner).wait_send()
        for d in range(1, S):
            cols_in((cz + d) % S, fi_send.at[d]).wait_send()
        for d in range(1, 16):
            ox, oz, _ = in_slab(d)
            block_in(ox, oz, pf_send.at[d], partner).wait_send()

    @pl.when(cy == 0)
    def _():
      for q in range(1, S):
          for copy in scatter(q):
              copy.wait_send()

    for d in range(1, S):
      for copy in stage_a(d, cx, cy):
          copy.wait_send()
    for d in range(1, S):
      for copy in stage_b(d, cx, cy):
          copy.wait_send()


def product_kernel(w, x_ref, r0, r1, o_hbm, o, o_sem):
    row, col = lax.axis_index("row"), lax.axis_index("col")
    wide = 2 * B
    parts = [pl.ds(j * wide, wide) for j in range(w.shape[1] // wide)]
    stores = [pltpu.make_async_copy(o.at[:, p], o_hbm.at[:, p], o_sem.at[j]) for j, p in enumerate(parts)]

    def right_operand(s, j):
        lanes = pl.ds(j % 2 * wide, wide)
        quarters = [(r0[q, s, :, lanes] if j < 2 else r1[s, q, :, lanes]) for q in range(S)]
        return jnp.concatenate(enc_right(jnp.concatenate(quarters, 0).astype(F32) - 1.0), 0)

    lefts = []
    for s in range(S):
        (f0, c0), (f1, c1) = enc_left(x_ref[s].astype(F32))
        lefts.append((f0, f1, c0, c1))
    for j, p in enumerate(parts):
        floors = ceils = None
        for s in range(S):
            right = right_operand(s, j)
            f0, f1, c0, c1 = (dot(left, right) for left in lefts[s])
            df, dc = jnp.maximum(f0, f1), jnp.maximum(c0, c1)
            floors = df if floors is None else jnp.maximum(floors, df)
            ceils = dc if ceils is None else jnp.maximum(ceils, dc)
        old = w[:, p]
        new = jnp.minimum(old.astype(F32), decode(floors, ceils, 2.0)).astype(jnp.int32)
        lag = lax.broadcasted_iota(jnp.int32, old.shape, 1) - lax.broadcasted_iota(jnp.int32, old.shape, 0)
        o[:, p] = jnp.where(lag == row * w.shape[0] - col * w.shape[1] - j * wide, 0, new)
        stores[j].start()
    for store in stores:
        store.wait()


def per_device(weights):
    dma = pltpu.SemaphoreType.DMA
    vmem = pl.BlockSpec(memory_space=pltpu.VMEM)
    rows, cols = weights.shape
    closed, r0, r1 = pl.pallas_call(
        gather_kernel,
        out_shape=(
            jax.ShapeDtypeStruct((S, rows, B), BF16),
            jax.ShapeDtypeStruct((S, S, 32, 512), BF16),
            jax.ShapeDtypeStruct((S, S, 32, 512), BF16),
        ),
        in_specs=[pl.BlockSpec(memory_space=pltpu.HBM)],
        out_specs=(vmem, vmem, vmem),
        scratch_shapes=[
            pltpu.VMEM((B, B), jnp.int32),
            pltpu.VMEM((B, cols), jnp.int32),
            pltpu.VMEM((rows, B), jnp.int32),
            pltpu.VMEM((S, 2, 32, 512), BF16),
            pltpu.VMEM((S, S, B, B), BF16),
            pltpu.VMEM((S, rows, B), BF16),
            pltpu.VMEM((2, 1024, 2 * B), F32),
            pltpu.VMEM((2, 2, 2 * B, 2 * B), BF16),
            dma((3,)), dma((S,)), dma, dma((16,)), dma((16,)), dma((16,)), dma((S,)), dma((S,)), dma((S,)),
            dma((S,)), dma, dma((S,)), dma,
            dma((S,)), dma((S,)), dma((S,)), dma((S,)), dma((S,)), dma((S,)), dma((S,)), dma((S,)),
        ],
        compiler_params=pltpu.CompilerParams(
            collective_id=0, has_side_effects=True, vmem_limit_bytes=24 * 2**20
        ),
        name="gather",
    )(pltpu.with_memory_space_constraint(weights, pltpu.HBM))
    return pl.pallas_call(
        product_kernel,
        out_shape=jax.ShapeDtypeStruct(weights.shape, jnp.int32),
        in_specs=[vmem] * 4,
        out_specs=pl.BlockSpec(memory_space=pltpu.HBM),
        scratch_shapes=[
            pltpu.VMEM((rows, cols), jnp.int32),
            dma((4,)),
        ],
        compiler_params=pltpu.CompilerParams(vmem_limit_bytes=32 * 2**20),
        name="product",
    )(weights, closed, r0, r1)


def solution(mesh):
    return jax.shard_map(
        per_device, mesh=mesh, in_specs=(P("row", "col"),), out_specs=P("row", "col"), check_vma=False
    )
```

profile of v0, /device:TPU:1, one launch (start us, length us, event | category | flops | bytes accessed | tf_op | source)
XLA Modules:
  0.0 34.6 jit_solution(3249703105057004026)
XLA Ops:
  0.0 0.0 copy-start
  0.0 28.3 %gather.1 = (bf16[4,512,128]{2,1,0:T(8,128)(2,1)S(1)}, bf16[4,4,32,512]{3,2,1,0:T(8,128)(2,1)S(1)}, bf16[4,4,32,512]{3,2,1,0:T(8,128)(2,1)S(1)}) custom-call(s32[512,1024]{1,0:T(8,128)} %w.1), custom_call_target="tpu_custom_call" | custom-call | tf_op jit(solution)/shard_map/gather/pallas_call | solution.py:407
  28.3 0.0 copy-done
  28.3 6.3 %product.1 = s32[512,1024]{1,0:T(8,128)} custom-call(s32[512,1024]{1,0:T(8,128)S(1)} %copy-done, bf16[4,512,128]{2,1,0:T(8,128)(2,1)S(1)} %get-tuple-element.8.x_ref, bf16[4,4,32,512]{3,2,1,0:T(8,128)(2,1)S(1)} %get-tuple-element.9.r0, bf16[4,4,32,512]{3,2,1,0:T(8,128)(2,1)S(1)} %get-tuple-element.10.r1), custom_call_target="tpu_custom_call" | custom-call | tf_op jit(solution)/shard_map/product/pallas_call | solution.py:434
Async XLA Ops:
  0.0 28.3 %copy-start = (s32[512,1024]{1,0:T(8,128)S(1)}, s32[512,1024]{1,0:T(8,128)}, u32[]{:S(2)}) copy-start(s32[512,1024]{1,0:T(8,128)} %w.1) | copy-start | bytes 6291460
where the time goes:
time: 34.7 us; the launch traced here: 34.6 us
  Pallas kernels  34.6 us (100%)
    pallas_call x1, Pallas kernels, per_device(): pl.pallas_call(gather_kernel, out_shape=(jax.ShapeDtypeStruct((S, rows, B...  28.3 us
    pallas_call x1, Pallas kernels, per_device(): pl.pallas_call(product_kernel, out_shape=jax.ShapeDtypeStruct(weights.sha...  6.26 us

commit v1 on v0

--- a/solution.py
+++ b/solution.py
@@ -284,6 +284,8 @@
             enc_row[s % 2, u, B : 2 * B, :] = floor
 
     start_b(0)
+    for t in range(S):
+        y[t // 2, S * B :, t % 2 * B : (t % 2 + 1) * B] = yi[t].astype(F32) - 1.0
 
     @pl.when(here != 0)
     def _():
@@ -312,7 +314,6 @@
         lanes = slice(t % 2 * B, (t % 2 + 1) * B)
         for s in range(S):
             y[t // 2, s * B : (s + 1) * B, lanes] = yp[t, s].astype(F32) - 1.0
-        y[t // 2, S * B :, lanes] = yi[t].astype(F32) - 1.0
 
     for s in range(S - 1):
         panel(s, block)

time: 34.7 us -> 34.8 us (level)
  no operation moved by 1% of the time
where the time goes in v1:
time: 34.8 us; the launch traced here: 34.6 us
  Pallas kernels  34.6 us (99%)
    pallas_call x1, Pallas kernels, per_device(): pl.pallas_call(gather_kernel, out_shape=(jax.ShapeDtypeStruct((S, rows, B...  28.3 us
    pallas_call x1, Pallas kernels, per_device(): pl.pallas_call(product_kernel, out_shape=jax.ShapeDtypeStruct(weights.sha...  6.26 us

profile of v1, /device:TPU:1, one launch (start us, length us, event | category | flops | bytes accessed | tf_op | source)
XLA Modules:
  0.0 34.6 jit_solution(4035101754104328389)
XLA Ops:
  0.0 0.0 copy-start
  0.0 28.3 %gather.1 = (bf16[4,512,128]{2,1,0:T(8,128)(2,1)S(1)}, bf16[4,4,32,512]{3,2,1,0:T(8,128)(2,1)S(1)}, bf16[4,4,32,512]{3,2,1,0:T(8,128)(2,1)S(1)}) custom-call(s32[512,1024]{1,0:T(8,128)} %w.1), custom_call_target="tpu_custom_call" | custom-call | tf_op jit(solution)/shard_map/gather/pallas_call | solution.py:408
  28.3 0.0 copy-done
  28.3 6.3 %product.1 = s32[512,1024]{1,0:T(8,128)} custom-call(s32[512,1024]{1,0:T(8,128)S(1)} %copy-done, bf16[4,512,128]{2,1,0:T(8,128)(2,1)S(1)} %get-tuple-element.8.x_ref, bf16[4,4,32,512]{3,2,1,0:T(8,128)(2,1)S(1)} %get-tuple-element.9.r0, bf16[4,4,32,512]{3,2,1,0:T(8,128)(2,1)S(1)} %get-tuple-element.10.r1), custom_call_target="tpu_custom_call" | custom-call | tf_op jit(solution)/shard_map/product/pallas_call | solution.py:435
Async XLA Ops:
  0.0 28.3 %copy-start = (s32[512,1024]{1,0:T(8,128)S(1)}, s32[512,1024]{1,0:T(8,128)}, u32[]{:S(2)}) copy-start(s32[512,1024]{1,0:T(8,128)} %w.1) | copy-start | bytes 6291460
